TPU v7x, 32 devices: a whole 2x2x4 slice. The times are simulated.
32 devices in a mesh: mkt: 8 (over z, x), grp: 4 (over y, core).
Axes of the slice: x: 2, y: 2, z: 4, core: 2. Of those that a mesh axis runs over, the one named last changes fastest.
Arguments:
- mean_utility: float32 [512, 64], P(('mkt', 'grp')), may hold values from -5 to -1
- market_share: float32 [512, 64], P(('mkt', 'grp')), may hold values from 0.001 to 0.02
- product_traits: float32 [512, 64, 5], P(('mkt', 'grp')), may hold values from -1 to 1
- taste_draws: float32 [512, 5, 1024], P(('mkt', 'grp')), may hold values from -4 to 4
- taste_scale: float32 [5], replicated, may hold values from 0.3 to 1
- type_weight: float32 [512, 1024], P(('mkt', 'grp')), may hold values from 0.1 to 1
- market_size: float32 [512], P(('mkt', 'grp')), may hold values from 0.05 to 3
- product_firm: int32 [512, 64], P(('mkt', 'grp')), may hold values from 0 to 511, all different within a row
- firm_order: int32 [512], replicated, may hold values from 0 to 511, each once
- loyalty: float32 [512, 1024], P(('mkt', 'grp')), may hold values from -1 to 1
- firm_share: float32 [512, 1024], replicated, may hold values from 2e-05 to 0.15
Outputs:
- utility_out: float32 [512, 64], P(('mkt', 'grp'))
- loyalty_out: float32 [512, 1024], P(('mkt', 'grp'))
Inputs may be any that keep to these rules, and one draw needn't show every extreme that they name: `product_firm`: in each market the 64 products belong to 64 different firms, and every firm sells in some market. `firm_order`: each firm appears once.
All inputs are finite; a program needn't handle non-finite values.
Results may differ from a plain program's by a relative error of at most 0.0001.
Values sent between devices are 32-bit elements; how exact they have to be, the bound alone decides.
A program may use at most 64 MiB of HBM per device.

v0:
```python
import jax
import jax.numpy as jnp
from jax import lax
from jax.sharding import PartitionSpec as P

ITERS = 3
clip_target = 0.5
norm_eps = 1e-06


def inverse_order(firm_order):
    count = firm_order.shape[0]
    return jnp.zeros((count,), jnp.int32).at[firm_order].set(jnp.arange(count, dtype=jnp.int32))


def market_terms(mean_now, taste, type_weight, mass, row_ids, table):
    expu = jnp.exp(mean_now[:, :, None] + taste + jnp.take(table, row_ids, axis=0))
    choice_prob = expu / (1.0 + jnp.sum(expu, axis=1, keepdims=True))
    weighted_sum = jnp.einsum(
        "mjr,mr->mj", choice_prob, type_weight, precision=lax.Precision.HIGHEST
    )
    weighted = choice_prob * mass[:, None, :]
    firm_count = table.shape[0]
    onehot = (
        jnp.arange(firm_count, dtype=jnp.int32)[:, None] == row_ids.reshape(-1)[None, :]
    ).astype(jnp.float32)
    partial_value = jnp.dot(
        onehot,
        weighted.reshape(-1, weighted.shape[2]),
        precision=lax.Precision.HIGHEST,
        preferred_element_type=jnp.float32,
    )
    return (weighted_sum, partial_value)


def local(
    mean_utility,
    market_share,
    product_traits,
    taste_draws,
    taste_scale,
    type_weight,
    market_size,
    product_firm,
    firm_order,
    loyalty,
    firm_share,
):
    firm_count = firm_share.shape[0]
    draw_count = firm_share.shape[1]
    owned_count = loyalty.shape[0]
    devices = lax.axis_size(("mkt", "grp"))
    inverse = inverse_order(firm_order)
    owner_rows = jnp.take(inverse, product_firm, axis=0)
    owned = loyalty
    my_firms = lax.dynamic_slice_in_dim(
        firm_order, lax.axis_index(("mkt", "grp")) * owned_count, owned_count
    )
    taste = jnp.einsum(
        "mjk,mkr->mjr", product_traits * taste_scale, taste_draws, precision=lax.Precision.HIGHEST
    )
    weight_total = jnp.sum(type_weight, axis=1)
    mass = market_size[:, None] * type_weight
    type_mass = lax.psum(jnp.sum(mass, axis=0), ("mkt", "grp"))
    log_observed = jnp.log(market_share)
    mean_now = mean_utility
    my_share = jnp.log(jnp.take(firm_share, my_firms, axis=0))
    for step in range(ITERS):
        table = lax.all_gather(owned, ("mkt", "grp"), axis=0, tiled=True)
        weighted_sum, by_owner = market_terms(mean_now, taste, type_weight, mass, owner_rows, table)
        predicted = weighted_sum / weight_total[:, None]
        blocks = by_owner.reshape(devices, owned_count, draw_count)
        received = lax.all_to_all(blocks, ("mkt", "grp"), split_axis=0, concat_axis=0, tiled=True)
        own_totals = jnp.sum(received, axis=0)
        gap = my_share - jnp.log(own_totals / type_mass[None, :])
        squares = lax.psum(jnp.sum(gap * gap), ("mkt", "grp"))
        clip = jnp.minimum(
            1.0, clip_target / jnp.sqrt(squares / (firm_count * draw_count) + norm_eps)
        )
        owned = owned + clip * gap
        mean_now = mean_now + log_observed - jnp.log(predicted)
    return (mean_now, owned)


def solution(mesh):
    placed = (
        P(("mkt", "grp"), None),
        P(("mkt", "grp"), None),
        P(("mkt", "grp"), None, None),
        P(("mkt", "grp"), None, None),
        P(),
        P(("mkt", "grp"), None),
        P(("mkt", "grp")),
        P(("mkt", "grp"), None),
        P(),
        P(("mkt", "grp"), None),
        P(),
    )
    return jax.shard_map(
        local,
        mesh=mesh,
        in_specs=placed,
        out_specs=(P(("mkt", "grp"), None), P(("mkt", "grp"), None)),
        check_vma=False,
    )
```

profile of v0, /device:TPU:12, one launch (start us, length us, event | category | flops | bytes accessed | tf_op | source)
XLA Modules:
  0.0 555.5 jit_solution(14951167932557971051)
XLA Ops:
  11.9 6.9 %gather_fusion = s32[1024]{0:T(1024)S(1)} fusion(s32[512]{0:T(512)S(1)} %scatter_custom_fusion, s32[1024]{0:T(1024)S(1)} %broadcast_clamp_fusion.1), kind=kCustom, calls=%fused_computation.3 | custom fusion | bytes 12288 | tf_op jit(solution)/shard_map/jit(_take)/gather | solution.py:54
  19.1 48.2 %all-gather.4.cloned.1.call-done = f32[512,1024]{1,0:T(8,128)} async-done(((f32[16,1024]{1,0:T(8,128)}), f32[512,1024]{1,0:T(8,128)}) %all-gather.4.cloned.1.call-update) | async-done | bytes 2097168 | tf_op jit(solution)/shard_map/all_gather | solution.py:69
  67.3 8.0 %gather_fusion.2 = f32[1024,1024]{1,0:T(8,128)} fusion(f32[512,1024]{1,0:T(8,128)} %all-gather.4.cloned.1.call-done, s32[1024]{0:T(1024)S(1)} %broadcast_clamp_fusion), kind=kCustom, calls=%fused_computation.clone | custom fusion | bytes 8392704 | tf_op jit(solution)/shard_map/jit(_take)/gather | solution.py:17
  75.3 7.5 %fusion.31 = (f32[16,1024]{1,0:T(8,128)S(1)}, f32[16,64,1024]{2,1,0:T(8,128)S(1)}, f32[16,64,1024]{2,1,0:T(8,128)}) fusion(f32[16,64,1024]{2,1,0:T(8,128)} %bitcast.24, pred[16,64]{1,0:T(8,128)(4,1)S(1)} %get-tuple-element.19, f32[16,64]{1,0:T(8,128)S(1)} %copy-done.11, f32[16,5,1024]{2,0,1:T(8,128)S(1)} %copy-done.4, ...), kind=kOutput, calls=%fused_computation.73 | convolution fusion | flops 67092480 | bytes 13001728 | tf_op jit(solution)/shard_map/mjk,mkr->mjr/dot_general | solution.py:59
  85.2 5.0 fusion.7
  90.2 4.7 all-to-all-start
  96.4 66.8 %psum.28 = f32[1024]{0:T(1024)S(1)} all-reduce(f32[1024]{0:T(1024)S(1)} %get-tuple-element.15), channel_id=1, replica_groups=mesh['mkt'=8,'grp'=4] {'mkt','grp'}, use_global_device_ids=true, to_apply=%region_5.7 | all-reduce | flops 1024 | bytes 8192 | tf_op jit(solution)/shard_map/psum | solution.py:64
  165.6 40.8 %psum.29 = f32[]{:T(128)} all-reduce(f32[]{:T(128)} %get-tuple-element.11), channel_id=1, replica_groups=mesh['mkt'=8,'grp'=4] {'mkt','grp'}, use_global_device_ids=true, to_apply=%region_7.9 | all-reduce | flops 1 | bytes 8 | tf_op jit(solution)/shard_map/psum | solution.py:76
  207.9 5.5 fusion.9
  213.6 49.5 %all-gather.6.cloned.1.call-done = f32[512,1024]{1,0:T(8,128)} async-done(((f32[16,1024]{1,0:T(8,128)}), f32[512,1024]{1,0:T(8,128)}) %all-gather.6.cloned.1.call-update) | async-done | bytes 2097168 | tf_op jit(solution)/shard_map/all_gather | solution.py:69
  263.0 8.0 %gather_fusion.3 = f32[1024,1024]{1,0:T(8,128)} fusion(f32[512,1024]{1,0:T(8,128)} %all-gather.6.cloned.1.call-done, s32[1024]{0:T(1024)S(1)} %broadcast_clamp_fusion), kind=kCustom, calls=%fused_computation.1.clone | custom fusion | bytes 8392704 | tf_op jit(solution)/shard_map/jit(_take)/gather | solution.py:17
  271.0 4.0 fusion.28
  277.4 3.7 fusion.5
  281.2 51.7 %all_to_all.15 = f32[32,16,1024]{2,1,0:T(8,128)} all-to-all(f32[32,16,1024]{2,1,0:T(8,128)S(1)} %fusion.5), channel_id=1, replica_groups=mesh['mkt'=8,'grp'=4] {'mkt','grp'}, dimensions={0} | all-to-all | bytes 4194304 | tf_op jit(solution)/shard_map/all_to_all | solution.py:73
  335.3 41.9 %psum.30 = f32[]{:T(128)} all-reduce(f32[]{:T(128)} %get-tuple-element.7), channel_id=1, replica_groups=mesh['mkt'=8,'grp'=4] {'mkt','grp'}, use_global_device_ids=true, to_apply=%region_11.13 | all-reduce | flops 1 | bytes 8 | tf_op jit(solution)/shard_map/psum | solution.py:76
  378.5 5.5 fusion.10
  384.1 48.1 %all-gather.8.cloned.1.call-done = f32[512,1024]{1,0:T(8,128)} async-done(((f32[16,1024]{1,0:T(8,128)}), f32[512,1024]{1,0:T(8,128)}) %all-gather.8.cloned.1.call-update) | async-done | bytes 2097168 | tf_op jit(solution)/shard_map/all_gather | solution.py:69
  432.2 8.0 %gather_fusion.4 = f32[1024,1024]{1,0:T(8,128)} fusion(f32[512,1024]{1,0:T(8,128)} %all-gather.8.cloned.1.call-done, s32[1024]{0:T(1024)S(1)} %broadcast_clamp_fusion), kind=kCustom, calls=%fused_computation.2.clone | custom fusion | bytes 8392704 | tf_op jit(solution)/shard_map/jit(_take)/gather | solution.py:17
  440.3 4.1 fusion.26
  446.6 5.0 fusion.3
  451.7 4.7 all-to-all-start.2
  456.4 5.5 fusion.11
  462.7 40.2 %all-to-all-done.2 = f32[32,16,1024]{2,1,0:T(8,128)} async-done(((f32[32,16,1024]{2,1,0:T(8,128)}), f32[32,16,1024]{2,1,0:T(8,128)}, u32[]{:S(2)}, u32[]{:S(2)}) %all-to-all-start.2) | async-done | bytes 2097184 | tf_op jit(solution)/shard_map/all_to_all | solution.py:73
  505.3 42.4 %psum.31 = f32[]{:T(128)} all-reduce(f32[]{:T(128)} %get-tuple-element.3), channel_id=1, replica_groups=mesh['mkt'=8,'grp'=4] {'mkt','grp'}, use_global_device_ids=true, to_apply=%region_15.17 | all-reduce | flops 1 | bytes 8 | tf_op jit(solution)/shard_map/psum | solution.py:76
  (72 shorter events, 23.7 us)
Async XLA Ops:
  7.2 88.6 %copy-start = (f32[512,1024]{1,0:T(8,128)S(1)}, f32[512,1024]{1,0:T(8,128)}, u32[]{:S(2)}) copy-start(f32[512,1024]{1,0:T(8,128)} %param.23) | copy-start | bytes 6291460
  7.2 60.1 %all-gather.4.cloned.1.call-start = ((), (), s32[]{:S(2)}) async-start(), calls=%async_computation.3 | async-start | bytes 2162688 | tf_op jit(solution)/shard_map/all_gather | solution.py:69
  11.8 7.0 %copy-start.12 = (s32[16,64]{1,0:T(8,128)S(1)}, s32[16,64]{1,0:T(8,128)}, u32[]{:S(2)}) copy-start(s32[16,64]{1,0:T(8,128)} %param.20) | copy-start | bytes 12292
  11.8 7.1 %copy-start.10 = (f32[16,64,5]{1,0,2:T(8,128)S(1)}, f32[16,64,5]{1,0,2:T(8,128)}, u32[]{:S(2)}) copy-start(f32[16,64,5]{1,0,2:T(8,128)} %param.15) | copy-start | bytes 61444
  11.9 7.1 %copy-start.13 = (f32[5]{0:T(128)S(1)}, f32[5]{0:T(128)}, u32[]{:S(2)}) copy-start(f32[5]{0:T(128)} %param.17) | copy-start | bytes 64
  19.1 56.2 %copy-start.4 = (f32[16,5,1024]{2,0,1:T(8,128)S(1)}, f32[16,5,1024]{2,0,1:T(8,128)}, u32[]{:S(2)}) copy-start(f32[16,5,1024]{2,0,1:T(8,128)} %param.16) | copy-start | bytes 983044
  19.1 56.2 %copy-start.11 = (f32[16,64]{1,0:T(8,128)S(1)}, f32[16,64]{1,0:T(8,128)}, u32[]{:S(2)}) copy-start(f32[16,64]{1,0:T(8,128)} %param.13) | copy-start | bytes 12292
  75.3 7.5 %copy-start.9 = (f32[16,1024]{1,0:T(8,128)S(1)}, f32[16,1024]{1,0:T(8,128)}, u32[]{:S(2)}) copy-start(f32[16,1024]{1,0:T(8,128)} %param.18) | copy-start | bytes 196612
  75.3 7.5 %copy-start.14 = (f32[16]{0:T(128)S(1)}, f32[16]{0:T(128)}, u32[]{:S(2)}) copy-start(f32[16]{0:T(128)} %param.19) | copy-start | bytes 196
  82.9 2.4 copy-start.1
  90.2 116.8 %copy-start.7 = (f32[16,1024]{1,0:T(8,128)S(1)}, f32[16,1024]{1,0:T(8,128)}, u32[]{:S(2)}) copy-start(f32[16,1024]{1,0:T(8,128)} %param.22) | copy-start | bytes 196612
  90.2 72.9 %all-to-all-start = ((f32[32,16,1024]{2,1,0:T(8,128)}), f32[32,16,1024]{2,1,0:T(8,128)}, u32[]{:S(2)}, u32[]{:S(2)}) async-start(f32[32,16,1024]{2,1,0:T(8,128)} %fusion.7), calls=%async_computation | async-start | bytes 4194304 | tf_op jit(solution)/shard_map/all_to_all | solution.py:73
  95.0 168.1 %all-gather.6.cloned.1.call-start = ((), (), s32[]{:S(2)}) async-start(), calls=%async_computation.4 | async-start | bytes 2162688 | tf_op jit(solution)/shard_map/all_gather | solution.py:69
  207.7 224.5 %all-gather.8.cloned.1.call-start = ((), (), s32[]{:S(2)}) async-start(), calls=%async_computation.5 | async-start | bytes 2162688 | tf_op jit(solution)/shard_map/all_gather | solution.py:69
  207.9 5.5 copy-start.8
  275.1 2.3 copy-start.2
  281.2 96.7 %copy-start.6 = (f32[16,1024]{1,0:T(8,128)S(1)}, f32[16,1024]{1,0:T(8,128)}, u32[]{:S(2)}) copy-start(f32[16,1024]{1,0:T(8,128)} %multiply_add_fusion.2) | copy-start | bytes 196612
  444.3 2.3 copy-start.3
  451.7 51.2 %all-to-all-start.2 = ((f32[32,16,1024]{2,1,0:T(8,128)}), f32[32,16,1024]{2,1,0:T(8,128)}, u32[]{:S(2)}, u32[]{:S(2)}) async-start(f32[32,16,1024]{2,1,0:T(8,128)} %fusion.3), calls=%async_computation.2 | async-start | bytes 4194304 | tf_op jit(solution)/shard_map/all_to_all | solution.py:73
  456.4 91.9 %copy-start.5 = (f32[16,1024]{1,0:T(8,128)S(1)}, f32[16,1024]{1,0:T(8,128)}, u32[]{:S(2)}) copy-start(f32[16,1024]{1,0:T(8,128)} %multiply_add_fusion.1) | copy-start | bytes 196612
Sparse Core Ops, SparseCore 0:
  10.8 56.4 all-gather.3
  207.8 55.1 all-gather.5
  378.7 53.5 all-gather.7
where the time goes:
time: 557 us; the launch traced here: 556 us
  blocking collectives  244 us (44%)
  waiting for transfers between devices  187 us (34%)
  local copies, waits for them, and re-layouts  38.1 us (7%)
  matrix products  37.9 us (7%)
  other arithmetic  23.5 us (4%)
  between operations  16 us (3%)
  starting transfers between devices  9.77 us (2%)
    all_gather x3, waiting for transfers between devices, local(): table = lax.all_gather(owned, ('mkt', 'grp'), axis=0, tiled=True)  146 us
    psum x3, blocking collectives, local(): squares = lax.psum(jnp.sum(gap * gap), ('mkt', 'grp'))  125 us
    psum x1, blocking collectives, local(): type_mass = lax.psum(jnp.sum(mass, axis=0), ('mkt', 'grp'))  66.8 us
    all_to_all x1, blocking collectives, local(): lax.all_to_all(blocks, ('mkt', 'grp'), split_axis=0, concat_axis=0, tiled...  51.7 us
    all_to_all x2, waiting for transfers between devices, local(): lax.all_to_all(blocks, ('mkt', 'grp'), split_axis=0, concat_axis=0, tiled...  40.2 us
    gather x3, local copies, waits for them, and re-layouts, market_terms(): jnp.take(table, row_ids, axis=0)  24 us
    dot_general x3, matrix products, market_terms(): jnp.einsum('mjr,mr->mj', choice_prob, type_weight, precision=lax.Precisio...  16.6 us
    dot_general x3, matrix products, market_terms(): jnp.dot(onehot, weighted.reshape(-1, weighted.shape[2]), precision=lax.Pr...  13.8 us
  transfers between devices with their start and end apart: 5, of which 4 were waited for; matrix products, arithmetic and copies ran while one was open for 5% of the time, Pallas kernels for 0%

commit v1 on v0

--- a/solution.py
+++ b/solution.py
@@ -66,7 +66,15 @@
     mean_now = mean_utility
     my_share = jnp.log(jnp.take(firm_share, my_firms, axis=0))
     for step in range(ITERS):
-        table = lax.all_gather(owned, ("mkt", "grp"), axis=0, tiled=True)
+        table = jnp.concatenate(
+            lax.all_to_all(
+                jnp.stack(lax.axis_size(("mkt", "grp")) * [owned], 0),
+                split_axis=0,
+                axis_name=("mkt", "grp"),
+                concat_axis=0,
+            ),
+            0,
+        )
         weighted_sum, by_owner = market_terms(mean_now, taste, type_weight, mass, owner_rows, table)
         predicted = weighted_sum / weight_total[:, None]
         blocks = by_owner.reshape(devices, owned_count, draw_count)

time: 557 us -> 530 us (0.952)
  waiting for transfers between devices: 187 us -> 158 us
  starting transfers between devices: 9.77 us -> 26.8 us
  between operations: 16 us -> 3.03 us
    all_gather x3 -> x0, waiting for transfers between devices: 146 us -> none  [local(): table = lax.all_gather(owned, ('mkt', 'grp'), axis=0, tiled=True)]
    all_to_all x0 -> x3, waiting for transfers between devices: none -> 118 us  [local(): lax.all_to_all(jnp.stack(lax.axis_size(('mkt', 'grp')) * [owned], 0), spl...]
    all_to_all x0 -> x3, starting transfers between devices: none -> 14 us  [local(): lax.all_to_all(jnp.stack(lax.axis_size(('mkt', 'grp')) * [owned], 0), spl...]
    another operation x0 -> x3, local copies, waits for them, and re-layouts: none -> 5.82 us  [local(): jnp.stack(lax.axis_size(('mkt', 'grp')) * [owned], 0)]
where the time goes in v1:
time: 530 us; the launch traced here: 529 us
  blocking collectives  246 us (46%)
  waiting for transfers between devices  158 us (30%)
  local copies, waits for them, and re-layouts  38.8 us (7%)
  matrix products  38 us (7%)
  starting transfers between devices  26.8 us (5%)
  other arithmetic  18.5 us (3%)
    psum x3, blocking collectives, local(): squares = lax.psum(jnp.sum(gap * gap), ('mkt', 'grp'))  125 us
    all_to_all x3, waiting for transfers between devices, local(): lax.all_to_all(jnp.stack(lax.axis_size(('mkt', 'grp')) * [owned], 0), spl...  118 us
    psum x1, blocking collectives, local(): type_mass = lax.psum(jnp.sum(mass, axis=0), ('mkt', 'grp'))  67.5 us
    all_to_all x1, blocking collectives, local(): lax.all_to_all(blocks, ('mkt', 'grp'), split_axis=0, concat_axis=0, tiled...  53.2 us
    all_to_all x2, waiting for transfers between devices, local(): lax.all_to_all(blocks, ('mkt', 'grp'), split_axis=0, concat_axis=0, tiled...  40.1 us
    gather x3, local copies, waits for them, and re-layouts, market_terms(): jnp.take(table, row_ids, axis=0)  18.9 us
    dot_general x3, matrix products, market_terms(): jnp.einsum('mjr,mr->mj', choice_prob, type_weight, precision=lax.Precisio...  16.7 us
    all_to_all x3, starting transfers between devices, local(): lax.all_to_all(jnp.stack(lax.axis_size(('mkt', 'grp')) * [owned], 0), spl...  14 us
  transfers between devices with their start and end apart: 5, of which 4 were waited for; matrix products, arithmetic and copies ran while one was open for 5% of the time, Pallas kernels for 0%

profile of v1, /device:TPU:12, one launch (start us, length us, event | category | flops | bytes accessed | tf_op | source)
XLA Modules:
  0.0 528.9 jit_solution(6874136523686788930)
XLA Ops:
  3.2 6.0 %all-to-all-start = ((f32[32,16,1024]{2,1,0:T(8,128)}), f32[32,16,1024]{2,1,0:T(8,128)}, u32[]{:S(2)}, u32[]{:S(2)}) async-start(f32[32,16,1024]{2,1,0:T(8,128)} %stack.6), calls=%async_computation | async-start | bytes 4194304 | tf_op jit(solution)/shard_map/all_to_all | solution.py:70
  11.8 6.9 %gather_fusion = s32[1024]{0:T(1024)S(1)} fusion(s32[512]{0:T(512)S(1)} %scatter_custom_fusion, s32[1024]{0:T(1024)S(1)} %broadcast_clamp_fusion.1), kind=kCustom, calls=%fused_computation.3 | custom fusion | bytes 12288 | tf_op jit(solution)/shard_map/jit(_take)/gather | solution.py:54
  19.0 36.6 %all-to-all-done = f32[32,16,1024]{2,1,0:T(8,128)} async-done(((f32[32,16,1024]{2,1,0:T(8,128)}), f32[32,16,1024]{2,1,0:T(8,128)}, u32[]{:S(2)}, u32[]{:S(2)}) %all-to-all-start) | async-done | bytes 2097184 | tf_op jit(solution)/shard_map/all_to_all | solution.py:70
  55.7 8.1 %gather_fusion.2 = f32[1024,1024]{1,0:T(8,128)} fusion(f32[512,1024]{1,0:T(8,128)} %bitcast, s32[1024]{0:T(1024)S(1)} %broadcast_clamp_fusion), kind=kCustom, calls=%fused_computation.clone | custom fusion | bytes 8392704 | tf_op jit(solution)/shard_map/jit(_take)/gather | solution.py:17
  63.8 7.5 %fusion.31 = (f32[16,1024]{1,0:T(8,128)S(1)}, f32[16,64,1024]{2,1,0:T(8,128)S(1)}, f32[16,64,1024]{2,1,0:T(8,128)}) fusion(f32[16,64,1024]{2,1,0:T(8,128)} %bitcast.29, pred[16,64]{1,0:T(8,128)(4,1)S(1)} %get-tuple-element.19, f32[16,64]{1,0:T(8,128)S(1)} %copy-done.10, f32[16,5,1024]{2,0,1:T(8,128)S(1)} %copy-done.5, ...), kind=kOutput, calls=%fused_computation.73 | convolution fusion | flops 67092480 | bytes 13001728 | tf_op jit(solution)/shard_map/mjk,mkr->mjr/dot_general | solution.py:59
  73.7 5.0 fusion.7
  78.7 6.4 %all-to-all-start.1 = ((f32[32,16,1024]{2,1,0:T(8,128)}), f32[32,16,1024]{2,1,0:T(8,128)}, u32[]{:S(2)}, u32[]{:S(2)}) async-start(f32[32,16,1024]{2,1,0:T(8,128)} %fusion.7), calls=%async_computation.1 | async-start | bytes 4194304 | tf_op jit(solution)/shard_map/all_to_all | solution.py:81
  85.8 67.5 %psum.28 = f32[1024]{0:T(1024)S(1)} all-reduce(f32[1024]{0:T(1024)S(1)} %get-tuple-element.15), channel_id=1, replica_groups=mesh['mkt'=8,'grp'=4] {'mkt','grp'}, use_global_device_ids=true, to_apply=%region_5.7 | all-reduce | flops 1024 | bytes 8192 | tf_op jit(solution)/shard_map/psum | solution.py:64
  155.7 40.7 %psum.29 = f32[]{:T(128)} all-reduce(f32[]{:T(128)} %get-tuple-element.11), channel_id=1, replica_groups=mesh['mkt'=8,'grp'=4] {'mkt','grp'}, use_global_device_ids=true, to_apply=%region_7.9 | all-reduce | flops 1 | bytes 8 | tf_op jit(solution)/shard_map/psum | solution.py:84
  198.7 4.8 all-to-all-start.2
  203.5 5.5 %fusion.9 = f32[16,1,64]{2,1,0:T(1,128)S(1)} fusion(f32[16,64,1024]{2,1,0:T(8,128)} %copy-done.2, f32[16,1024]{1,0:T(8,128)S(1)} %get-tuple-element.23, f32[16,1024,1]{1,0,2:T(8,128)S(1)} %bitcast.33), kind=kOutput, calls=%fused_computation.24 | convolution fusion | flops 13631488 | bytes 4329472 | tf_op jit(solution)/shard_map/mjr,mr->mj/dot_general | solution.py:19
  209.1 40.8 %all-to-all-done.2 = f32[32,16,1024]{2,1,0:T(8,128)S(1)} async-done(((f32[32,16,1024]{2,1,0:T(8,128)}), f32[32,16,1024]{2,1,0:T(8,128)S(1)}, u32[]{:S(2)}, u32[]{:S(2)}) %all-to-all-start.2) | async-done | bytes 2097184 | tf_op jit(solution)/shard_map/all_to_all | solution.py:70
  249.9 5.4 %gather_fusion.3 = f32[1024,1024]{1,0:T(8,128)} fusion(f32[512,1024]{1,0:T(8,128)S(1)} %bitcast.28, s32[1024]{0:T(1024)S(1)} %broadcast_clamp_fusion), kind=kCustom, calls=%fused_computation.1.clone | custom fusion | bytes 8392704 | tf_op jit(solution)/shard_map/jit(_take)/gather | solution.py:17
  265.4 53.2 %all_to_all.30 = f32[32,16,1024]{2,1,0:T(8,128)S(1)} all-to-all(f32[32,16,1024]{2,1,0:T(8,128)S(1)} %fusion.5), channel_id=1, replica_groups=mesh['mkt'=8,'grp'=4] {'mkt','grp'}, dimensions={0} | all-to-all | bytes 4194304 | tf_op jit(solution)/shard_map/all_to_all | solution.py:81
  319.5 41.7 %psum.30 = f32[]{:T(128)} all-reduce(f32[]{:T(128)} %get-tuple-element.7), channel_id=1, replica_groups=mesh['mkt'=8,'grp'=4] {'mkt','grp'}, use_global_device_ids=true, to_apply=%region_11.13 | all-reduce | flops 1 | bytes 8 | tf_op jit(solution)/shard_map/psum | solution.py:84
  366.7 5.5 %fusion.10 = f32[16,1,64]{2,1,0:T(1,128)S(1)} fusion(f32[16,64,1024]{2,1,0:T(8,128)} %copy-done.3, f32[16,1024]{1,0:T(8,128)S(1)} %broadcast_add_fusion.1, f32[16,1024,1]{1,0,2:T(8,128)S(1)} %bitcast.34), kind=kOutput, calls=%fused_computation.25 | convolution fusion | flops 13631488 | bytes 4329472 | tf_op jit(solution)/shard_map/mjr,mr->mj/dot_general | solution.py:19
  372.3 40.8 %all-to-all-done.4 = f32[32,16,1024]{2,1,0:T(8,128)S(1)} async-done(((f32[32,16,1024]{2,1,0:T(8,128)}), f32[32,16,1024]{2,1,0:T(8,128)S(1)}, u32[]{:S(2)}, u32[]{:S(2)}) %all-to-all-start.4) | async-done | bytes 2097184 | tf_op jit(solution)/shard_map/all_to_all | solution.py:70
  413.1 5.4 %gather_fusion.4 = f32[1024,1024]{1,0:T(8,128)} fusion(f32[512,1024]{1,0:T(8,128)S(1)} %bitcast.27, s32[1024]{0:T(1024)S(1)} %broadcast_clamp_fusion), kind=kCustom, calls=%fused_computation.2.clone | custom fusion | bytes 8392704 | tf_op jit(solution)/shard_map/jit(_take)/gather | solution.py:17
  418.5 4.0 fusion.26
  424.9 5.0 fusion.3
  429.9 6.4 %all-to-all-start.5 = ((f32[32,16,1024]{2,1,0:T(8,128)}), f32[32,16,1024]{2,1,0:T(8,128)}, u32[]{:S(2)}, u32[]{:S(2)}) async-start(f32[32,16,1024]{2,1,0:T(8,128)} %fusion.3), calls=%async_computation.5 | async-start | bytes 4194304 | tf_op jit(solution)/shard_map/all_to_all | solution.py:81
  436.3 5.7 %fusion.11 = f32[16,1,64]{2,1,0:T(1,128)S(1)} fusion(f32[16,64,1024]{2,1,0:T(8,128)} %copy-done.4, f32[16,1024]{1,0:T(8,128)S(1)} %broadcast_add_fusion, f32[16,1024,1]{1,0,2:T(8,128)S(1)} %bitcast.35), kind=kOutput, calls=%fused_computation.26 | convolution fusion | flops 13631488 | bytes 4329472 | tf_op jit(solution)/shard_map/mjr,mr->mj/dot_general | solution.py:19
  442.7 40.1 %all-to-all-done.5 = f32[32,16,1024]{2,1,0:T(8,128)} async-done(((f32[32,16,1024]{2,1,0:T(8,128)}), f32[32,16,1024]{2,1,0:T(8,128)}, u32[]{:S(2)}, u32[]{:S(2)}) %all-to-all-start.5) | async-done | bytes 2097184 | tf_op jit(solution)/shard_map/all_to_all | solution.py:81
  485.2 42.4 %psum.31 = f32[]{:T(128)} all-reduce(f32[]{:T(128)} %get-tuple-element.3), channel_id=1, replica_groups=mesh['mkt'=8,'grp'=4] {'mkt','grp'}, use_global_device_ids=true, to_apply=%region_15.17 | all-reduce | flops 1 | bytes 8 | tf_op jit(solution)/shard_map/psum | solution.py:84
  (72 shorter events, 34.4 us)
Async XLA Ops:
  0.6 84.5 %copy-start = (f32[512,1024]{1,0:T(8,128)S(1)}, f32[512,1024]{1,0:T(8,128)}, u32[]{:S(2)}) copy-start(f32[512,1024]{1,0:T(8,128)} %param.23) | copy-start | bytes 6291460
  0.6 8.6 %copy-start.11 = (s32[16,64]{1,0:T(8,128)S(1)}, s32[16,64]{1,0:T(8,128)}, u32[]{:S(2)}) copy-start(s32[16,64]{1,0:T(8,128)} %param.20) | copy-start | bytes 12292
  0.7 8.7 %copy-start.12 = (s32[512]{0:T(512)S(1)}, s32[512]{0:T(512)}, u32[]{:S(2)}) copy-start(s32[512]{0:T(512)} %param.21) | copy-start | bytes 6148
  3.2 52.5 %all-to-all-start = ((f32[32,16,1024]{2,1,0:T(8,128)}), f32[32,16,1024]{2,1,0:T(8,128)}, u32[]{:S(2)}, u32[]{:S(2)}) async-start(f32[32,16,1024]{2,1,0:T(8,128)} %stack.6), calls=%async_computation | async-start | bytes 4194304 | tf_op jit(solution)/shard_map/all_to_all | solution.py:70
  11.8 7.1 %copy-start.9 = (f32[16,64,5]{1,0,2:T(8,128)S(1)}, f32[16,64,5]{1,0,2:T(8,128)}, u32[]{:S(2)}) copy-start(f32[16,64,5]{1,0,2:T(8,128)} %param.15) | copy-start | bytes 61444
  11.8 7.1 %copy-start.13 = (f32[5]{0:T(128)S(1)}, f32[5]{0:T(128)}, u32[]{:S(2)}) copy-start(f32[5]{0:T(128)} %param.17) | copy-start | bytes 64
  55.7 8.1 %copy-start.5 = (f32[16,5,1024]{2,0,1:T(8,128)S(1)}, f32[16,5,1024]{2,0,1:T(8,128)}, u32[]{:S(2)}) copy-start(f32[16,5,1024]{2,0,1:T(8,128)} %param.16) | copy-start | bytes 983044
  55.7 8.1 %copy-start.10 = (f32[16,64]{1,0:T(8,128)S(1)}, f32[16,64]{1,0:T(8,128)}, u32[]{:S(2)}) copy-start(f32[16,64]{1,0:T(8,128)} %param.13) | copy-start | bytes 12292
  63.8 7.5 %copy-start.8 = (f32[16,1024]{1,0:T(8,128)S(1)}, f32[16,1024]{1,0:T(8,128)}, u32[]{:S(2)}) copy-start(f32[16,1024]{1,0:T(8,128)} %param.18) | copy-start | bytes 196612
  63.8 7.5 %copy-start.14 = (f32[16]{0:T(128)S(1)}, f32[16]{0:T(128)}, u32[]{:S(2)}) copy-start(f32[16]{0:T(128)} %param.19) | copy-start | bytes 196
  71.3 2.4 copy-start.2
  78.7 118.4 %copy-start.6 = (f32[16,1024]{1,0:T(8,128)S(1)}, f32[16,1024]{1,0:T(8,128)}, u32[]{:S(2)}) copy-start(f32[16,1024]{1,0:T(8,128)} %param.22) | copy-start | bytes 196612
  78.7 74.6 %all-to-all-start.1 = ((f32[32,16,1024]{2,1,0:T(8,128)}), f32[32,16,1024]{2,1,0:T(8,128)}, u32[]{:S(2)}, u32[]{:S(2)}) async-start(f32[32,16,1024]{2,1,0:T(8,128)} %fusion.7), calls=%async_computation.1 | async-start | bytes 4194304 | tf_op jit(solution)/shard_map/all_to_all | solution.py:81
  198.7 51.2 %all-to-all-start.2 = ((f32[32,16,1024]{2,1,0:T(8,128)}), f32[32,16,1024]{2,1,0:T(8,128)S(1)}, u32[]{:S(2)}, u32[]{:S(2)}) async-start(f32[32,16,1024]{2,1,0:T(8,128)} %stack.7), calls=%async_computation.2 | async-start | bytes 4194304 | tf_op jit(solution)/shard_map/all_to_all | solution.py:70
  203.5 5.5 %copy-start.7 = (f32[16,64]{1,0:T(8,128)S(1)}, f32[16,64]{1,0:T(8,128)}, u32[]{:S(2)}) copy-start(f32[16,64]{1,0:T(8,128)} %param.14) | copy-start | bytes 12292
  259.4 2.3 copy-start.3
  363.5 49.5 %all-to-all-start.4 = ((f32[32,16,1024]{2,1,0:T(8,128)}), f32[32,16,1024]{2,1,0:T(8,128)S(1)}, u32[]{:S(2)}, u32[]{:S(2)}) async-start(f32[32,16,1024]{2,1,0:T(8,128)} %stack.8), calls=%async_computation.4 | async-start | bytes 4194304 | tf_op jit(solution)/shard_map/all_to_all | solution.py:70
  422.6 2.3 copy-start.4
  429.9 52.8 %all-to-all-start.5 = ((f32[32,16,1024]{2,1,0:T(8,128)}), f32[32,16,1024]{2,1,0:T(8,128)}, u32[]{:S(2)}, u32[]{:S(2)}) async-start(f32[32,16,1024]{2,1,0:T(8,128)} %fusion.3), calls=%async_computation.5 | async-start | bytes 4194304 | tf_op jit(solution)/shard_map/all_to_all | solution.py:81
  436.3 92.6 %copy-start.1 = (f32[512,1024]{1,0:T(8,128)S(1)}, f32[512,1024]{1,0:T(8,128)}, u32[]{:S(2)}) copy-start(f32[512,1024]{1,0:T(8,128)} %param.23) | copy-start | bytes 6291460
